TPU v7x, 32 devices: a whole 2x2x4 slice. The times are simulated.
32 devices in a mesh: gx: 16 (over z, y, core), gy: 2 (over x).
Axes of the slice: x: 2, y: 2, z: 4, core: 2. Of those that a mesh axis runs over, the one named last changes fastest.
Arguments:
- fluid_velocity: float32 [3, 64, 32, 128], P(None, 'gx', 'gy'), may hold values from -6 to 6
- particle_velocity: float32 [16, 2, 4, 3, 128], P('gx', 'gy'), may hold values from -6 to 6
- particle_volume: float32 [16, 2, 4, 128], P('gx', 'gy'), may hold values from 0.02 to 0.3
- satellite_cells: int32 [16, 2, 4, 29, 128], P('gx', 'gy'), may hold values from 0 to 13823
- live_blocks: int32 [16, 2], P('gx', 'gy'), may hold values from 1 to 4
Outputs:
- void_fraction: float32 [64, 32, 128], P('gx', 'gy')
- drag: float32 [16, 2, 4, 3, 128], P('gx', 'gy')
Inputs may be any that keep to these rules, and one draw needn't show every extreme that they name: `live_blocks`: blocks from this number on hold no live particles.
All inputs are finite; a program needn't handle non-finite values.
Results may differ from a plain program's by a relative error of at most 0.00029.
Values sent between devices are 32-bit elements; how exact they have to be, the bound alone decides.
A program may use at most 64 MiB of HBM per device.

v0:
```python
import math

import jax
import jax.numpy as jnp
from jax import lax
from jax.sharding import PartitionSpec as P

exponent = -2.65
drag_scale = 2.0
void_floor = 0.1


def passed_along(value, axis, steps):
    count = lax.axis_size(axis)
    pairs = [(source, (source + steps) % count) for source in range(count)]
    return lax.ppermute(value, axis, pairs)


def padded(cells, sides, width):
    for axis, dim in sides:
        count = lax.axis_size(axis)
        head = lax.slice_in_dim(cells, 0, width, axis=dim)
        tail = lax.slice_in_dim(cells, cells.shape[dim] - width, cells.shape[dim], axis=dim)
        cells = jnp.concatenate(
            [
                lax.ppermute(tail, axis, [(i, (i + 1) % count) for i in range(count)]),
                cells,
                lax.ppermute(head, axis, [((i + 1) % count, i) for i in range(count)]),
            ],
            axis=dim,
        )
    return cells


def body(fluid_velocity, particle_velocity, particle_volume, satellite_cells, live_blocks):
    cells_x = fluid_velocity.shape[1]
    cells_y = fluid_velocity.shape[2]
    cells_z = fluid_velocity.shape[3]
    wide_x = cells_x + 2
    wide_y = cells_y + 2
    satellites = satellite_cells[0, 0]
    volume = particle_volume[0, 0]
    velocity = particle_velocity[0, 0]
    live_count = live_blocks[0, 0]
    block_count = satellites.shape[0]
    point_count = satellites.shape[1]
    lane_count = satellites.shape[2]
    group_size = math.gcd(block_count, 8)
    turns = (live_count + group_size - 1) // group_size

    def group_share(group_index):
        start = group_index * group_size
        alive = (start + jnp.arange(group_size, dtype=jnp.int32) < live_count).astype(jnp.float32)
        return volume * alive[:, None] / point_count

    def deposit(group_index, deposit_tile):
        start = group_index * group_size
        weights = jnp.broadcast_to(group_share(group_index)[:, None, :], satellites.shape)
        return deposit_tile.at[satellites.reshape(-1)].add(weights.reshape(-1))

    empty_tile = jnp.zeros((wide_x * wide_y * cells_z,), jnp.float32)
    deposit_tile = lax.fori_loop(0, turns, deposit, empty_tile).reshape(wide_x, wide_y, cells_z)
    below_x = passed_along(deposit_tile[-1], "gx", 1)
    above_x = passed_along(deposit_tile[0], "gx", -1)
    interior = deposit_tile[1:-1].at[0].add(below_x).at[-1].add(above_x)
    below_y = passed_along(interior[:, -1], "gy", 1)
    above_y = passed_along(interior[:, 0], "gy", -1)
    solid_volume = interior[:, 1:-1].at[:, 0].add(below_y).at[:, -1].add(above_y)
    void_fraction = jnp.maximum(1.0 - solid_volume, void_floor)
    stacked = jnp.concatenate([fluid_velocity, void_fraction[None]], axis=0)
    fields_wide = padded(stacked, (("gx", 1), ("gy", 2)), 1)
    velocity_wide = fields_wide[:3]
    void_wide = fields_wide[3]
    resistance = (void_wide**exponent).reshape(-1)
    flow = velocity_wide.reshape(3, -1)

    def drag_group(group_index, drag_out):
        start = group_index * group_size
        volume_share = group_share(group_index)
        weight_at = jnp.take(resistance, satellites)
        flow_at = jnp.take(flow, satellites, axis=1)
        weight_sum = jnp.sum(weight_at, axis=1)
        pulling = jnp.transpose(jnp.sum(weight_at[None] * flow_at, axis=2), (1, 0, 2))
        force = (
            drag_scale * volume_share[:, None, :] * (pulling - velocity * weight_sum[:, None, :])
        )
        return force

    empty_drag = jnp.zeros((block_count, 3, lane_count), jnp.float32)
    drag_out = lax.fori_loop(0, turns, drag_group, empty_drag)
    return (void_fraction, drag_out[None, None])


def solution(mesh):
    placed = (
        P(None, "gx", "gy", None),
        P("gx", "gy", None, None, None),
        P("gx", "gy", None, None),
        P("gx", "gy", None, None, None),
        P("gx", "gy"),
    )
    return jax.shard_map(
        body,
        mesh=mesh,
        in_specs=placed,
        out_specs=(P("gx", "gy", None), P("gx", "gy", None, None, None)),
        check_vma=False,
    )
```

profile of v0, /device:TPU:0, one launch (start us, length us, event | category | flops | bytes accessed | tf_op | source)
XLA Modules:
  0.0 228.3 jit_solution(16518074461500624984)
XLA Ops:
  1.3 0.8 copy.21
  2.1 0.0 copy-start.1
  2.1 0.1 reshape_squeeze.3
  2.2 0.5 copy-done.1
  2.7 0.0 copy-start.4
  2.8 0.0 copy-start
  2.8 82.1 %while.29 = (s32[]{:T(128)}, f32[13824]{0:T(1024)S(1)}, s32[]{:T(128)}, s32[1,1,4,29,128]{4,3,2,1,0:T(8,128)}, s32[]{:T(128)}, /*index=5*/f32[4,128]{1,0:T(4,128)}, s32[14848,1]{0,1:T(1,128)S(1)}, s32[]{:T(128)}, s32[]{:T(128)}) while((s32[]{:T(128)}, f32[13824]{0:T(1024)S(1)}, s32[]{:T(128)}, s32[1,1,4,29,128]{4,3,2,1,0:T(8,128)}, ...), condition=%wide.wide.region_2.3_spmd, body=%wide.wide.region_0.2_spmd.sunk | while | flops 60431 | bytes 540817 | solution.py:62
  2.8 0.7 compare_convert_fusion.6
  3.5 0.8 multiply_multiply_fusion.6
  4.2 0.2 fusion.13
  4.4 80.4 %scatter_fusion = f32[13824]{0:T(1024)S(1)} fusion(f32[13824]{0:T(1024)S(1)} %get-tuple-element.434, s32[14848]{0:T(1024)S(1)} %fusion.13, f32[14848]{0:T(1024)S(1)} %reshape.357), kind=kCustom, calls=%fused_computation.2.clone.clone.1 | custom fusion | flops 14848 | bytes 237568 | tf_op jit(solution)/shard_map/while/body/scatter-add | solution.py:59
  84.9 1.2 collective-permute-start
  86.1 4.5 %collective-permute-start.1 = (f32[18,128]{1,0:T(8,128)S(1)}, f32[18,128]{1,0:T(8,128)S(1)}, u32[]{:S(2)}, u32[]{:S(2)}) collective-permute-start(f32[18,128]{1,0:T(8,128)S(1)} %get-tuple-element.300), channel_id=1, source_target_pairs={{0,30},{2,0},{4,2},{6,4},{8,6},{10,8},{12,10},{14,12},{16,14},{18,... | collective-permute-start | bytes 27656 | tf_op jit(solution)/shard_map/ppermute | solution.py:16
  90.6 1.3 collective-permute-done
  91.9 0.1 collective-permute-done.1
  92.0 1.3 collective-permute-start.2
  93.3 0.0 copy-done.4
  93.3 0.9 collective-permute-start.3
  94.3 1.4 collective-permute-done.2
  95.7 1.3 collective-permute-done.3
  97.1 0.1 collective-permute-start.4
  97.1 4.4 %collective-permute-start.5 = (f32[4,1,16,128]{3,2,1,0:T(8,128)S(1)}, f32[4,1,16,128]{3,2,1,0:T(8,128)S(1)}, u32[]{:S(2)}, u32[]{:S(2)}) collective-permute-start(f32[4,1,16,128]{3,2,1,0:T(8,128)S(1)} %get-tuple-element.299), channel_id=1, source_target_pairs={{2,0},{4,2},{6,4},{8,6},{10,8},{12,10},{14,12},{16,14},{18,16},{20... | collective-permute-start | bytes 98312 | tf_op jit(solution)/shard_map/ppermute | solution.py:28
  101.6 0.0 copy-done
  101.6 1.5 collective-permute-done.4
  103.1 0.0 collective-permute-done.5
  103.2 0.9 collective-permute-start.6
  104.1 1.2 collective-permute-start.7
  105.3 0.6 copy.30
  105.9 1.0 collective-permute-done.6
  106.9 0.8 collective-permute-done.7
  107.8 0.1 maximum_power_fusion
  107.8 76.4 %gather_fusion = f32[14848]{0:T(1024)S(1)} fusion(f32[13824]{0:T(1024)S(1)} %pow.12, s32[15360]{0:T(1024)S(1)} %pad_clamp_fusion), kind=kCustom, calls=%fused_computation | custom fusion | bytes 178176 | tf_op jit(solution)/shard_map/while/body/jit(_take)/gather | solution.py:80
  184.4 0.0 copy-start.2
  184.4 0.0 copy-start.3
  184.4 4.3 %copy.28 = f32[3,6,18,128]{0,3,2,1:T(8,128)} copy(f32[3,6,18,128]{3,2,1,0:T(8,128)S(1)} %pad_maximum_fusion) | data formatting | bytes 331776 | tf_op jit(solution)/shard_map/slice | solution.py:72
  188.7 31.1 %gather_fusion.1 = f32[14848,3]{1,0:T(8,128)} fusion(f32[3,13824]{0,1:T(8,128)} %bitcast.48, s32[15360]{0:T(1024)S(1)} %pad_clamp_fusion), kind=kCustom, calls=%fused_computation.1 | custom fusion | bytes 415744 | tf_op jit(solution)/shard_map/while/body/jit(_take)/gather | solution.py:81
  219.8 6.5 %multiply_reduce_fusion = f32[4,128,3]{2,1,0:T(8,128)S(1)} fusion(f32[4,29,128,3]{3,2,1,0:T(8,128)} %bitcast.49, f32[4,29,128]{2,1,0:T(8,128)S(1)} %get-tuple-element.294, pred[4,29,128]{2,1,0:T(8,128)(4,1)S(1)} %get-tuple-element.295), kind=kLoop, calls=%fused_computation.11 | loop fusion | flops 132096 | bytes 258560 | tf_op jit(solution)/shard_map/while/body/reduce_sum | solution.py:83
  226.3 0.1 copy.29
  226.4 0.6 broadcast_in_dim.50
  227.0 0.0 copy-done.2
  227.0 0.0 copy-done.3
  227.0 1.3 while.28
  227.0 0.6 compare_convert_fusion.5
  227.7 0.1 multiply_multiply_fusion.5
  227.7 0.6 fusion.12
  (26 shorter events, 0.3 us)
Async XLA Ops:
  2.1 0.6 copy-start.1
  2.7 90.6 %copy-start.4 = (f32[3,4,16,128]{3,2,1,0:T(8,128)S(1)}, f32[3,4,16,128]{3,2,1,0:T(8,128)}, u32[]{:S(2)}) copy-start(f32[3,4,16,128]{3,2,1,0:T(8,128)} %param.17) | copy-start | bytes 294916
  2.8 98.8 %copy-start = (s32[1,1,4,29,128]{4,2,3,1,0:T(4,128)S(1)}, s32[1,1,4,29,128]{4,2,3,1,0:T(4,128)}, u32[]{:S(2)}) copy-start(s32[1,1,4,29,128]{4,2,3,1,0:T(4,128)} %param.20) | copy-start | bytes 178180
  84.9 7.0 %collective-permute-start = (f32[18,128]{1,0:T(8,128)S(1)}, f32[18,128]{1,0:T(8,128)S(1)}, u32[]{:S(2)}, u32[]{:S(2)}) collective-permute-start(f32[18,128]{1,0:T(8,128)S(1)} %get-tuple-element.301), channel_id=1, source_target_pairs={{0,2},{2,4},{4,6},{6,8},{8,10},{10,12},{12,14},{14,16},{16,18},{18... | collective-permute-start | bytes 27656 | tf_op jit(solution)/shard_map/ppermute | solution.py:16
  86.1 5.9 %collective-permute-start.1 = (f32[18,128]{1,0:T(8,128)S(1)}, f32[18,128]{1,0:T(8,128)S(1)}, u32[]{:S(2)}, u32[]{:S(2)}) collective-permute-start(f32[18,128]{1,0:T(8,128)S(1)} %get-tuple-element.300), channel_id=1, source_target_pairs={{0,30},{2,0},{4,2},{6,4},{8,6},{10,8},{12,10},{14,12},{16,14},{18,... | collective-permute-start | bytes 27656 | tf_op jit(solution)/shard_map/ppermute | solution.py:16
  92.0 3.7 %collective-permute-start.2 = (f32[4,128]{1,0:T(4,128)S(1)}, f32[4,128]{1,0:T(4,128)S(1)}, u32[]{:S(2)}, u32[]{:S(2)}) collective-permute-start(f32[4,128]{1,0:T(4,128)S(1)} %bitcast.56), channel_id=1, source_target_pairs={{0,1},{1,0},{2,3},{3,2},{4,5},{5,4},{6,7},{7,6},{8,9},{9,8},{10,11... | collective-permute-start | bytes 6152 | tf_op jit(solution)/shard_map/ppermute | solution.py:16
  93.3 3.7 %collective-permute-start.3 = (f32[4,128]{1,0:T(4,128)S(1)}, f32[4,128]{1,0:T(4,128)S(1)}, u32[]{:S(2)}, u32[]{:S(2)}) collective-permute-start(f32[4,128]{1,0:T(4,128)S(1)} %bitcast.55), channel_id=1, source_target_pairs={{0,1},{1,0},{2,3},{3,2},{4,5},{5,4},{6,7},{7,6},{8,9},{9,8},{10,11... | collective-permute-start | bytes 6152 | tf_op jit(solution)/shard_map/ppermute | solution.py:16
  97.1 6.1 %collective-permute-start.4 = (f32[4,1,16,128]{3,2,1,0:T(8,128)S(1)}, f32[4,1,16,128]{3,2,1,0:T(8,128)S(1)}, u32[]{:S(2)}, u32[]{:S(2)}) collective-permute-start(f32[4,1,16,128]{3,2,1,0:T(8,128)S(1)} %get-tuple-element.298), channel_id=1, source_target_pairs={{0,2},{2,4},{4,6},{6,8},{8,10},{10,12},{12,14},{14,16},{16,18},{18... | collective-permute-start | bytes 98312 | tf_op jit(solution)/shard_map/ppermute | solution.py:26
  97.1 6.0 %collective-permute-start.5 = (f32[4,1,16,128]{3,2,1,0:T(8,128)S(1)}, f32[4,1,16,128]{3,2,1,0:T(8,128)S(1)}, u32[]{:S(2)}, u32[]{:S(2)}) collective-permute-start(f32[4,1,16,128]{3,2,1,0:T(8,128)S(1)} %get-tuple-element.299), channel_id=1, source_target_pairs={{2,0},{4,2},{6,4},{8,6},{10,8},{12,10},{14,12},{16,14},{18,16},{20... | collective-permute-start | bytes 98312 | tf_op jit(solution)/shard_map/ppermute | solution.py:28
  103.2 3.8 %collective-permute-start.6 = (f32[4,6,1,128]{3,2,1,0:T(1,128)S(1)}, f32[4,6,1,128]{3,2,1,0:T(1,128)S(1)}, u32[]{:S(2)}, u32[]{:S(2)}) collective-permute-start(f32[4,6,1,128]{3,2,1,0:T(1,128)S(1)} %get-tuple-element.296), channel_id=1, source_target_pairs={{0,1},{1,0},{2,3},{3,2},{4,5},{5,4},{6,7},{7,6},{8,9},{9,8},{10,11... | collective-permute-start | bytes 36872 | tf_op jit(solution)/shard_map/ppermute | solution.py:26
  104.1 3.7 %collective-permute-start.7 = (f32[4,6,1,128]{3,2,1,0:T(1,128)S(1)}, f32[4,6,1,128]{3,2,1,0:T(1,128)S(1)}, u32[]{:S(2)}, u32[]{:S(2)}) collective-permute-start(f32[4,6,1,128]{3,2,1,0:T(1,128)S(1)} %get-tuple-element.297), channel_id=1, source_target_pairs={{1,0},{0,1},{3,2},{2,3},{5,4},{4,5},{7,6},{6,7},{9,8},{8,9},{11,10... | collective-permute-start | bytes 36872 | tf_op jit(solution)/shard_map/ppermute | solution.py:28
  184.4 42.7 %copy-start.2 = (f32[4,128]{1,0:T(4,128)S(1)}, f32[4,128]{1,0:T(4,128)}, u32[]{:S(2)}) copy-start(f32[4,128]{1,0:T(4,128)} %get-tuple-element.483) | copy-start | bytes 6148
  184.4 42.6 %copy-start.3 = (f32[1,1,4,3,128]{4,2,3,1,0:T(4,128)S(1)}, f32[1,1,4,3,128]{4,2,3,1,0:T(4,128)}, u32[]{:S(2)}) copy-start(f32[1,1,4,3,128]{4,2,3,1,0:T(4,128)} %param.18) | copy-start | bytes 18436
where the time goes:
time: 228 us
  local copies, waits for them, and re-layouts  115 us (50%)
  other arithmetic  90.1 us (40%)
  starting transfers between devices  14.5 us (6%)
  waiting for transfers between devices  7.54 us (3%)
    scatter-add x1, other arithmetic, deposit(): return deposit_tile.at[satellites.reshape(-1)].add(weights.reshape(-1))  80.4 us
    gather x2, local copies, waits for them, and re-layouts, drag_group(): weight_at = jnp.take(resistance, satellites)  76.4 us
    gather x1, local copies, waits for them, and re-layouts, drag_group(): flow_at = jnp.take(flow, satellites, axis=1)  31.1 us
    ppermute x4, starting transfers between devices, passed_along(): return lax.ppermute(value, axis, pairs)  7.88 us
    reduce_sum x1, other arithmetic, drag_group(): jnp.sum(weight_at[None] * flow_at, axis=2)  6.51 us
    ppermute x2, starting transfers between devices, padded(): lax.ppermute(head, axis, [((i + 1) % count, i) for i in range(count)])  5.62 us
  transfers between devices with their start and end apart: 8, of which 7 were waited for; matrix products, arithmetic and copies ran while one was open for 0% of the time, Pallas kernels for 0%

commit v1 on v0

v1 whole, which is shorter than its diff:
```python
import functools

import jax
import jax.numpy as jnp
from jax import lax
from jax.experimental import pallas as pl
from jax.experimental.pallas import tpu as pltpu
from jax.sharding import PartitionSpec as P

exponent = -2.65
drag_scale = 2.0
void_floor = 0.1

MESH = pl.DeviceIdType.MESH
DIRECTIONS = [(-1, 0), (1, 0), (0, -1), (0, 1), (-1, -1), (-1, 1), (1, -1), (1, 1)]


def rounded_up(count, unit):
    return (count + unit - 1) // unit * unit


def halves(value):
    high = value.astype(jnp.bfloat16)
    low = (value - high.astype(jnp.float32)).astype(jnp.bfloat16)
    return high, low


def kernel(
    sizes,
    live_ref,
    fluid_ref,
    velocity_ref,
    volume_ref,
    cells_ref,
    void_ref,
    drag_ref,
    spots,
    tile,
    wide,
    fields,
    out_x,
    out_y,
    out_c,
    in_x,
    in_y,
    in_c,
    flow_out_y,
    flow_out_c,
    flow_in_x,
    flow_in_y,
    flow_in_c,
    send_sem,
    recv_sem,
):
    count_x, count_y, cells_x, cells_y, pair, point_count = sizes
    wide_x, wide_y = cells_x + 2, cells_y + 2
    lanes = cells_ref.shape[-1]
    depth = tile.shape[1]
    rows = tile.shape[0]
    block_count = cells_ref.shape[0]
    turns = block_count // pair
    here_x, here_y = lax.axis_index("gx"), lax.axis_index("gy")

    def neighbour(direction):
        dx, dy = direction
        return (
            lax.rem(here_x + (dx + count_x), count_x),
            lax.rem(here_y + (dy + count_y), count_y),
        )

    barrier = pltpu.get_barrier_semaphore()
    for direction in DIRECTIONS:
        pl.semaphore_signal(barrier, inc=1, device_id=neighbour(direction), device_id_type=MESH)

    for side, j in enumerate((0, cells_y - 1)):
        for k in range(3):
            for i in range(cells_x):
                flow_out_y[side, k * cells_x + i : k * cells_x + i + 1] = fluid_ref[k, i, j : j + 1]
            for side_x, i in enumerate((0, cells_x - 1)):
                flow_out_c[side_x * 2 + side, k : k + 1] = fluid_ref[k, i, j : j + 1]

    alive_below = live_ref[0, 0]

    def shares(turn):
        parts = []
        for h in range(pair):
            block = turn * pair + h
            alive = jnp.where(
                jnp.full((1, lanes), block, jnp.int32) < alive_below, 1.0, 0.0
            )
            parts.append(volume_ref[pl.ds(block, 1), :] * alive / point_count)
        return jnp.concatenate(parts, axis=1)

    def cell_rows(turn, s):
        return jnp.concatenate(
            [cells_ref[turn * pair + h, s : s + 1, :] for h in range(pair)], axis=1
        )

    width = pair * lanes
    row_ids = lax.broadcasted_iota(jnp.int32, (rows, width), 0)
    depth_ids = lax.broadcasted_iota(jnp.int32, (depth, width), 0)

    def deposit(turn, total):
        high, low = halves(shares(turn))
        high, low = high.astype(jnp.float32), low.astype(jnp.float32)
        for s in range(point_count):
            cells = cell_rows(turn, s)
            spot = jnp.where(depth_ids == cells % depth, 1.0, 0.0).astype(jnp.bfloat16)
            spots[turn, s] = spot
            hit = row_ids == cells // depth
            weights = jnp.concatenate(
                [
                    jnp.where(hit, high, 0.0).astype(jnp.bfloat16),
                    jnp.where(hit, low, 0.0).astype(jnp.bfloat16),
                ],
                axis=0,
            )
            total = total + lax.dot_general(
                weights, spot, (((1,), (1,)), ((), ())), preferred_element_type=jnp.float32
            )
        return total

    total = jnp.zeros((2 * rows, depth), jnp.float32)
    first = turns // 2
    total = lax.fori_loop(0, first, deposit, total)

    pl.semaphore_wait(barrier, len(DIRECTIONS))

    def flow_copy(slot):
        dx, dy = DIRECTIONS[slot]
        side_x, side_y = int(dx > 0), int(dy > 0)
        if dy == 0:
            source, target = fluid_ref.at[:, side_x * (cells_x - 1)], flow_in_x.at[side_x]
        elif dx == 0:
            source, target = flow_out_y.at[side_y], flow_in_y.at[side_y]
        else:
            corner = side_x * 2 + side_y
            source, target = flow_out_c.at[corner], flow_in_c.at[corner]
        return pltpu.make_async_remote_copy(
            src_ref=source,
            dst_ref=target,
            send_sem=send_sem.at[8 + slot],
            recv_sem=recv_sem.at[8 + slot],
            device_id=neighbour(DIRECTIONS[slot]),
            device_id_type=MESH,
        )

    def volume_copy(slot):
        dx, dy = DIRECTIONS[slot]
        side_x, side_y = int(dx > 0), int(dy > 0)
        if dy == 0:
            source, target = out_x.at[side_x], in_x.at[side_x]
        elif dx == 0:
            source, target = out_y.at[side_y], in_y.at[side_y]
        else:
            corner = side_x * 2 + side_y
            source, target = out_c.at[corner], in_c.at[corner]
        return pltpu.make_async_remote_copy(
            src_ref=source,
            dst_ref=target,
            send_sem=send_sem.at[slot],
            recv_sem=recv_sem.at[slot],
            device_id=neighbour(DIRECTIONS[slot]),
            device_id_type=MESH,
        )

    for slot in range(8):
        flow_copy(slot).start()

    total = lax.fori_loop(first, turns, deposit, total)
    tile[...] = total[:rows] + total[rows:]

    band = 2 * wide_y
    top = (wide_x - 2) * wide_y
    out_x[0, :band] = tile[:band]
    out_x[1, :band] = tile[top : top + band]
    for side, j in enumerate((0, wide_y - 2)):
        for i in range(wide_x):
            out_y[side, 2 * i : 2 * i + 2] = tile[i * wide_y + j : i * wide_y + j + 2]
        for side_x, first_i in enumerate((0, wide_x - 2)):
            for step in range(2):
                start = (first_i + step) * wide_y + j
                out_c[side_x * 2 + side, 2 * step : 2 * step + 2] = tile[start : start + 2]

    for k in range(3):
        for i in range(cells_x):
            start = (i + 1) * wide_y + 1
            wide[k, start : start + cells_y] = fluid_ref[k, i]

    for slot in (4, 5, 6, 7, 0, 1, 2, 3):
        volume_copy(slot).start()

    spare = rows - wide_x * wide_y
    for k in range(3):
        if spare:
            wide[k, wide_x * wide_y :] = jnp.zeros((spare, depth), jnp.float32)
    for slot in range(8):
        flow_copy(slot).wait()
    for k in range(3):
        for side in range(2):
            i = wide_x - 1 if side == 0 else 0
            wide[k, i * wide_y + 1 : i * wide_y + 1 + cells_y] = flow_in_x[side, k]
            j = wide_y - 1 if side == 0 else 0
            for layer in range(cells_x):
                at = (layer + 1) * wide_y + j
                wide[k, at : at + 1] = flow_in_y[side, k * cells_x + layer : k * cells_x + layer + 1]
            for side_y in range(2):
                at = i * wide_y + (wide_y - 1 if side_y == 0 else 0)
                wide[k, at : at + 1] = flow_in_c[side * 2 + side_y, k : k + 1]

    for slot in range(8):
        volume_copy(slot).wait()
    tile[top : top + band] += in_x[0, :band]
    tile[:band] += in_x[1, :band]
    for side in range(2):
        j = wide_y - 2 if side == 0 else 0
        for i in range(wide_x):
            tile[i * wide_y + j : i * wide_y + j + 2] += in_y[side, 2 * i : 2 * i + 2]
        for side_x in range(2):
            first_i = wide_x - 2 if side_x == 0 else 0
            for step in range(2):
                start = (first_i + step) * wide_y + j
                tile[start : start + 2] += in_c[side_x * 2 + side, 2 * step : 2 * step + 2]

    void = jnp.maximum(1.0 - tile[...], void_floor)
    tile[...] = void
    resistance = jnp.exp(exponent * jnp.log(void))
    for k in range(4):
        high, low = halves(resistance * wide[k] if k < 3 else resistance)
        fields[k * rows : (k + 1) * rows, :depth] = high
        fields[k * rows : (k + 1) * rows, depth:] = low
    for i in range(cells_x):
        start = (i + 1) * wide_y + 1
        void_ref[i] = tile[start : start + cells_y]

    def pull(turn, carry):
        sums = [jnp.zeros((8, width), jnp.float32) for _ in range(4)]
        for s in range(point_count):
            spot = spots[turn, s]
            picked = jnp.dot(
                fields[...],
                jnp.concatenate([spot, spot], axis=0),
                preferred_element_type=jnp.float32,
            )
            hit = row_ids == cell_rows(turn, s) // depth
            for k in range(4):
                chosen = jnp.where(hit, picked[k * rows : (k + 1) * rows], 0.0)
                sums[k] = sums[k] + jnp.sum(chosen.reshape(rows // 8, 8, width), axis=0)
        share = shares(turn)
        weight_sum = jnp.sum(sums[3], axis=0, keepdims=True)
        for k in range(3):
            pulling = jnp.sum(sums[k], axis=0, keepdims=True)
            for h in range(pair):
                at = slice(h * lanes, (h + 1) * lanes)
                block = turn * pair + h
                drag_ref[block, k : k + 1] = (
                    drag_scale
                    * share[:, at]
                    * (pulling[:, at] - velocity_ref[block, k : k + 1] * weight_sum[:, at])
                )
        return carry

    lax.fori_loop(0, turns, pull, 0)


def body(fluid_velocity, particle_velocity, particle_volume, satellite_cells, live_blocks):
    _, cells_x, cells_y, depth = fluid_velocity.shape
    wide_x, wide_y = cells_x + 2, cells_y + 2
    satellites = satellite_cells[0, 0]
    block_count, point_count, lanes = satellites.shape
    pair = 2 if block_count % 2 == 0 else 1
    rows = rounded_up(wide_x * wide_y, 16)
    band = rounded_up(2 * wide_y, 8)
    sides = rounded_up(2 * wide_x, 8)
    flow_sides = rounded_up(3 * cells_x, 8)
    sizes = (lax.axis_size("gx"), lax.axis_size("gy"), cells_x, cells_y, pair, point_count)
    vmem = pl.BlockSpec(memory_space=pltpu.VMEM)
    f32 = jnp.float32
    void_fraction, drag = pl.pallas_call(
        functools.partial(kernel, sizes),
        out_shape=(
            jax.ShapeDtypeStruct((cells_x, cells_y, depth), f32),
            jax.ShapeDtypeStruct((block_count, 3, lanes), f32),
        ),
        in_specs=[pl.BlockSpec(memory_space=pltpu.SMEM), vmem, vmem, vmem, vmem],
        out_specs=(vmem, vmem),
        scratch_shapes=[
            pltpu.VMEM((block_count // pair, point_count, depth, pair * lanes), jnp.bfloat16),
            pltpu.VMEM((rows, depth), f32),
            pltpu.VMEM((3, rows, depth), f32),
            pltpu.VMEM((4 * rows, 2 * depth), jnp.bfloat16),
            pltpu.VMEM((2, band, depth), f32),
            pltpu.VMEM((2, sides, depth), f32),
            pltpu.VMEM((4, 8, depth), f32),
            pltpu.VMEM((2, band, depth), f32),
            pltpu.VMEM((2, sides, depth), f32),
            pltpu.VMEM((4, 8, depth), f32),
            pltpu.VMEM((2, flow_sides, depth), f32),
            pltpu.VMEM((4, 8, depth), f32),
            pltpu.VMEM((2, 3, cells_y, depth), f32),
            pltpu.VMEM((2, flow_sides, depth), f32),
            pltpu.VMEM((4, 8, depth), f32),
            pltpu.SemaphoreType.DMA((16,)),
            pltpu.SemaphoreType.DMA((16,)),
        ],
        compiler_params=pltpu.CompilerParams(collective_id=0, has_side_effects=True),
    )(live_blocks, fluid_velocity, particle_velocity[0, 0], particle_volume[0, 0], satellites)
    return void_fraction, drag[None, None]


def solution(mesh):
    placed = (
        P(None, "gx", "gy", None),
        P("gx", "gy", None, None, None),
        P("gx", "gy", None, None),
        P("gx", "gy", None, None, None),
        P("gx", "gy"),
    )
    return jax.shard_map(
        body,
        mesh=mesh,
        in_specs=placed,
        out_specs=(P("gx", "gy", None), P("gx", "gy", None, None, None)),
        check_vma=False,
    )
```

time: 228 us -> 24.7 us (0.11)
  local copies, waits for them, and re-layouts: 115 us -> 5.4 us
  other arithmetic: 90.1 us -> 0 us
  Pallas kernels: 0 us -> 17.6 us
  starting transfers between devices: 14.5 us -> 0 us
  waiting for transfers between devices: 7.54 us -> 0 us
    gather x3 -> x0, local copies, waits for them, and re-layouts: 107 us -> none  [the longest x2 76.4 us: drag_group(): weight_at = jnp.take(resistance, satellites)]
    scatter-add x5 -> x0, other arithmetic: 80.4 us -> none  [the longest x1 80.4 us: deposit(): return deposit_tile.at[satellites.reshape(-1)].add(weights.reshape(-1))]
    pallas_call x0 -> x1, Pallas kernels: none -> 17.6 us  [body(): pl.pallas_call(functools.partial(kernel, sizes), out_shape=(jax.ShapeDtyp...]
    ppermute x8 -> x0, starting transfers between devices: 14.5 us -> none  [the longest x4 7.88 us: passed_along(): return lax.ppermute(value, axis, pairs)]
    ppermute x8 -> x0, waiting for transfers between devices: 7.54 us -> none  [the longest x4 4.12 us: passed_along(): return lax.ppermute(value, axis, pairs)]
    reduce_sum x2 -> x0, other arithmetic: 6.55 us -> none  [the longest x1 6.51 us: drag_group(): jnp.sum(weight_at[None] * flow_at, axis=2)]
    slice x7 -> x0, local copies, waits for them, and re-layouts: 4.38 us -> none  [the longest x1 4.34 us: body(): velocity_wide = fields_wide[:3]]
    unnamed x13 -> x4, local copies, waits for them, and re-layouts: 1.2 us -> 5.4 us
  transfers between devices with their start and end apart: 8 -> 0, of which waited for: 7 -> 0; matrix products, arithmetic and copies ran while one was open for 0% -> 0% of each run, Pallas kernels for 0% -> 0%
where the time goes in v1:
time: 24.7 us; the launch traced here: 24.3 us
  Pallas kernels  17.6 us (71%)
  local copies, waits for them, and re-layouts  5.4 us (22%)
  between operations  1.29 us (5%)
    pallas_call x1, Pallas kernels, body(): pl.pallas_call(functools.partial(kernel, sizes), out_shape=(jax.ShapeDtyp...  17.6 us
    unnamed x4, local copies, waits for them, and re-layouts  5.4 us

profile of v1, /device:TPU:0, one launch (start us, length us, event | category | flops | bytes accessed | tf_op | source)
XLA Modules:
  0.0 24.3 jit_solution(16161784430184606356)
XLA Ops:
  1.3 1.3 %copy.13 = f32[1,1,4,3,128]{4,3,2,1,0:T(4,128)} copy(f32[1,1,4,3,128]{4,2,3,1,0:T(4,128)} %param.6) | data formatting | bytes 12288 | tf_op args[1]
  2.6 1.4 %copy.12 = s32[1,1,4,29,128]{4,3,2,1,0:T(8,128)} copy(s32[1,1,4,29,128]{4,2,3,1,0:T(4,128)} %param.8) | data formatting | bytes 118784 | tf_op args[3]
  4.0 17.6 %shard_map.68 = (f32[4,16,128]{2,1,0:T(8,128)}, f32[4,3,128]{2,1,0:T(4,128)}) custom-call(s32[1,1]{1,0:T(1,128)S(6)} %copy.15.live_ref, f32[3,4,16,128]{3,2,1,0:T(8,128)} %fluid_ref.1, f32[4,3,128]{2,1,0:T(4,128)} %bitcast.9, f32[4,128]{1,0:T(4,128)} %bitcast.11, s32[4,29,128]{2,1,0:T(8,128)} %bitcast.8), custom_call_target="tpu_custom_call" | custom-call | tf_op jit(solution)/shard_map/pallas_call | solution.py:279
  21.7 1.3 %copy.9 = f32[1,1,4,3,128]{4,2,3,1,0:T(4,128)} copy(f32[1,1,4,3,128]{4,3,2,1,0:T(4,128)} %bitcast.10) | data formatting | bytes 12288
  22.9 1.4 %copy.16 = f32[4,16,128]{2,1,0:T(8,128)} copy(f32[4,16,128]{2,1,0:T(8,128)} %get-tuple-element.10) | data formatting | bytes 65536

commit v2 on v1

--- a/solution.py
+++ b/solution.py
@@ -57,7 +57,7 @@
     lanes = cells_ref.shape[-1]
     depth = tile.shape[1]
     rows = tile.shape[0]
-    block_count = cells_ref.shape[0]
+    block_count = cells_ref.shape[1]
     turns = block_count // pair
     here_x, here_y = lax.axis_index("gx"), lax.axis_index("gy")
 
@@ -79,50 +79,61 @@
             for side_x, i in enumerate((0, cells_x - 1)):
                 flow_out_c[side_x * 2 + side, k : k + 1] = fluid_ref[k, i, j : j + 1]
 
-    alive_below = live_ref[0, 0]
+    alive_below = jnp.broadcast_to(live_ref[...], (1, lanes))
+    half = rows // 2
+    width = pair * lanes
 
     def shares(turn):
         parts = []
         for h in range(pair):
             block = turn * pair + h
-            alive = jnp.where(
-                jnp.full((1, lanes), block, jnp.int32) < alive_below, 1.0, 0.0
-            )
-            parts.append(volume_ref[pl.ds(block, 1), :] * alive / point_count)
+            alive = jnp.where(alive_below > block, 1.0, 0.0)
+            parts.append(volume_ref[block : block + 1, :] * alive / point_count)
         return jnp.concatenate(parts, axis=1)
 
     def cell_rows(turn, s):
         return jnp.concatenate(
-            [cells_ref[turn * pair + h, s : s + 1, :] for h in range(pair)], axis=1
+            [cells_ref[s, turn * pair + h : turn * pair + h + 1, :] for h in range(pair)], axis=1
         )
 
-    width = pair * lanes
-    row_ids = lax.broadcasted_iota(jnp.int32, (rows, width), 0)
-    depth_ids = lax.broadcasted_iota(jnp.int32, (depth, width), 0)
-
-    def deposit(turn, total):
+    def narrow_rows(row, count):
+        tall = jnp.broadcast_to(row.astype(jnp.float32), (16, width)).astype(jnp.bfloat16)
+        return jnp.concatenate([tall] * (count // 16), axis=0)
+
+    def narrow_ids(count):
+        return lax.broadcasted_iota(jnp.int32, (count, width), 0).astype(jnp.float32)
+
+    place_ids = narrow_ids(2 * depth).astype(jnp.bfloat16)
+    both_ids = jnp.concatenate([narrow_ids(half)] * 2, axis=0).astype(jnp.bfloat16)
+    one = jnp.ones((), jnp.bfloat16)
+    zero = jnp.zeros((), jnp.bfloat16)
+
+    def deposit(turn, totals):
         high, low = halves(shares(turn))
-        high, low = high.astype(jnp.float32), low.astype(jnp.float32)
+        split = jnp.concatenate(
+            [
+                jnp.broadcast_to(high.astype(jnp.float32), (half, width)),
+                jnp.broadcast_to(low.astype(jnp.float32), (half, width)),
+            ],
+            axis=0,
+        ).astype(jnp.bfloat16)
+        totals = list(totals)
         for s in range(point_count):
             cells = cell_rows(turn, s)
-            spot = jnp.where(depth_ids == cells % depth, 1.0, 0.0).astype(jnp.bfloat16)
+            spot = jnp.where(place_ids == narrow_rows(cells % (2 * depth), 2 * depth), one, zero)
             spots[turn, s] = spot
-            hit = row_ids == cells // depth
-            weights = jnp.concatenate(
-                [
-                    jnp.where(hit, high, 0.0).astype(jnp.bfloat16),
-                    jnp.where(hit, low, 0.0).astype(jnp.bfloat16),
-                ],
-                axis=0,
+            weights = jnp.where(
+                both_ids == narrow_rows(cells // (2 * depth), 2 * half), split, zero
             )
-            total = total + lax.dot_general(
+            totals[s % 2] = totals[s % 2] + lax.dot_general(
                 weights, spot, (((1,), (1,)), ((), ())), preferred_element_type=jnp.float32
             )
-        return total
-
-    total = jnp.zeros((2 * rows, depth), jnp.float32)
+        return totals
+
+    totals = [jnp.zeros((2 * half, 2 * depth), jnp.float32)] * 2
     first = turns // 2
-    total = lax.fori_loop(0, first, deposit, total)
+    for turn in range(first):
+        totals = deposit(turn, totals)
 
     pl.semaphore_wait(barrier, len(DIRECTIONS))
 
@@ -167,8 +178,13 @@
     for slot in range(8):
         flow_copy(slot).start()
 
-    total = lax.fori_loop(first, turns, deposit, total)
-    tile[...] = total[:rows] + total[rows:]
+    for turn in range(first, turns):
+        totals = deposit(turn, totals)
+    total = totals[0] + totals[1]
+    total = total[:half] + total[half:]
+    evens, odds = pl.ds(0, half, stride=2), pl.ds(1, half, stride=2)
+    tile[evens] = total[:, :depth]
+    tile[odds] = total[:, depth:]
 
     band = 2 * wide_y
     top = (wide_x - 2) * wide_y
@@ -224,16 +240,23 @@
 
     void = jnp.maximum(1.0 - tile[...], void_floor)
     tile[...] = void
+    void = jnp.concatenate([tile[evens], tile[odds]], axis=1)
     resistance = jnp.exp(exponent * jnp.log(void))
-    for k in range(4):
-        high, low = halves(resistance * wide[k] if k < 3 else resistance)
-        fields[k * rows : (k + 1) * rows, :depth] = high
-        fields[k * rows : (k + 1) * rows, depth:] = low
+    parts = [
+        resistance * jnp.concatenate([wide[k, evens], wide[k, odds]], axis=1) for k in range(3)
+    ] + [resistance]
+    mixed = jnp.concatenate(
+        [part[g * 8 : (g + 1) * 8] for g in range(half // 8) for part in parts], axis=0
+    )
+    high, low = halves(mixed)
+    fields[:, : 2 * depth] = high
+    fields[:, 2 * depth :] = low
     for i in range(cells_x):
         start = (i + 1) * wide_y + 1
         void_ref[i] = tile[start : start + cells_y]
 
-    def pull(turn, carry):
+    group_ids = lax.broadcasted_iota(jnp.int32, (8, width), 0)
+    for turn in range(turns):
         sums = [jnp.zeros((8, width), jnp.float32) for _ in range(4)]
         for s in range(point_count):
             spot = spots[turn, s]
@@ -242,10 +265,12 @@
                 jnp.concatenate([spot, spot], axis=0),
                 preferred_element_type=jnp.float32,
             )
-            hit = row_ids == cell_rows(turn, s) // depth
-            for k in range(4):
-                chosen = jnp.where(hit, picked[k * rows : (k + 1) * rows], 0.0)
-                sums[k] = sums[k] + jnp.sum(chosen.reshape(rows // 8, 8, width), axis=0)
+            row = jnp.broadcast_to(cell_rows(turn, s) // (2 * depth), (8, width))
+            for g in range(half // 8):
+                hit = row == group_ids + 8 * g
+                for k in range(4):
+                    at = (g * 4 + k) * 8
+                    sums[k] = sums[k] + jnp.where(hit, picked[at : at + 8], 0.0)
         share = shares(turn)
         weight_sum = jnp.sum(sums[3], axis=0, keepdims=True)
         for k in range(3):
@@ -253,14 +278,11 @@
             for h in range(pair):
                 at = slice(h * lanes, (h + 1) * lanes)
                 block = turn * pair + h
-                drag_ref[block, k : k + 1] = (
+                drag_ref[k, block : block + 1] = (
                     drag_scale
                     * share[:, at]
-                    * (pulling[:, at] - velocity_ref[block, k : k + 1] * weight_sum[:, at])
+                    * (pulling[:, at] - velocity_ref[k, block : block + 1] * weight_sum[:, at])
                 )
-        return carry
-
-    lax.fori_loop(0, turns, pull, 0)
 
 
 def body(fluid_velocity, particle_velocity, particle_volume, satellite_cells, live_blocks):
@@ -280,15 +302,15 @@
         functools.partial(kernel, sizes),
         out_shape=(
             jax.ShapeDtypeStruct((cells_x, cells_y, depth), f32),
-            jax.ShapeDtypeStruct((block_count, 3, lanes), f32),
+            jax.ShapeDtypeStruct((3, block_count, lanes), f32),
         ),
-        in_specs=[pl.BlockSpec(memory_space=pltpu.SMEM), vmem, vmem, vmem, vmem],
+        in_specs=[vmem] * 5,
         out_specs=(vmem, vmem),
         scratch_shapes=[
-            pltpu.VMEM((block_count // pair, point_count, depth, pair * lanes), jnp.bfloat16),
+            pltpu.VMEM((block_count // pair, point_count, 2 * depth, pair * lanes), jnp.bfloat16),
             pltpu.VMEM((rows, depth), f32),
             pltpu.VMEM((3, rows, depth), f32),
-            pltpu.VMEM((4 * rows, 2 * depth), jnp.bfloat16),
+            pltpu.VMEM((2 * rows, 4 * depth), jnp.bfloat16),
             pltpu.VMEM((2, band, depth), f32),
             pltpu.VMEM((2, sides, depth), f32),
             pltpu.VMEM((4, 8, depth), f32),
@@ -304,8 +326,14 @@
             pltpu.SemaphoreType.DMA((16,)),
         ],
         compiler_params=pltpu.CompilerParams(collective_id=0, has_side_effects=True),
-    )(live_blocks, fluid_velocity, particle_velocity[0, 0], particle_volume[0, 0], satellites)
-    return void_fraction, drag[None, None]
+    )(
+        live_blocks,
+        fluid_velocity,
+        jnp.swapaxes(particle_velocity[0, 0], 0, 1),
+        particle_volume[0, 0],
+        jnp.swapaxes(satellites, 0, 1),
+    )
+    return void_fraction, jnp.swapaxes(drag, 0, 1)[None, None]
 
 
 def solution(mesh):

time: 24.7 us -> 23 us (0.931)
  local copies, waits for them, and re-layouts: 5.4 us -> 1.98 us
  Pallas kernels: 17.6 us -> 19.5 us
    unnamed x4, local copies, waits for them, and re-layouts: 5.4 us -> 1.98 us
    pallas_call x1, Pallas kernels: 17.6 us -> 19.5 us  [body(): pl.pallas_call(functools.partial(kernel, sizes), out_shape=(jax.ShapeDtyp...]
where the time goes in v2:
time: 23 us; the launch traced here: 22.8 us
  Pallas kernels  19.5 us (85%)
  local copies, waits for them, and re-layouts  1.98 us (9%)
  between operations  1.29 us (6%)
    pallas_call x1, Pallas kernels, body(): pl.pallas_call(functools.partial(kernel, sizes), out_shape=(jax.ShapeDtyp...  19.5 us
    unnamed x4, local copies, waits for them, and re-layouts  1.98 us

profile of v2, /device:TPU:0, one launch (start us, length us, event | category | flops | bytes accessed | tf_op | source)
XLA Modules:
  0.0 22.8 jit_solution(18360188075789359416)
XLA Ops:
  1.3 19.5 %shard_map.68 = (f32[4,16,128]{2,1,0:T(8,128)}, f32[3,4,128]{2,1,0:T(4,128)}) custom-call(s32[1,1]{1,0:T(1,128)S(6)} %copy.9.live_ref, f32[3,4,16,128]{3,2,1,0:T(8,128)} %fluid_ref.1, f32[3,4,128]{2,1,0:T(4,128)} %bitcast.12, f32[4,128]{1,0:T(4,128)} %bitcast.13, s32[29,4,128]{2,1,0:T(4,128)} %bitcast.10), custom_call_target="tpu_custom_call" | custom-call | tf_op jit(solution)/shard_map/pallas_call | solution.py:301
  20.8 0.0 copy-start
  20.8 1.4 %copy.10 = f32[4,16,128]{2,1,0:T(8,128)} copy(f32[4,16,128]{2,1,0:T(8,128)} %get-tuple-element.8) | data formatting | bytes 65536
  22.2 0.0 copy-done
  22.2 0.6 %copy.11 = f32[1,1,4,3,128]{4,2,3,1,0:T(4,128)} copy(f32[1,1,4,3,128]{4,2,3,1,0:T(4,128)S(1)} %bitcast.11) | data formatting | bytes 12288
Async XLA Ops:
  20.8 1.4 %copy-start = (f32[3,4,128]{2,1,0:T(4,128)S(1)}, f32[3,4,128]{2,1,0:T(4,128)}, u32[]{:S(2)}) copy-start(f32[3,4,128]{2,1,0:T(4,128)} %get-tuple-element.5) | copy-start | bytes 18436

commit v3 on v2

--- a/solution.py
+++ b/solution.py
@@ -28,12 +28,17 @@
 def kernel(
     sizes,
     live_ref,
+    fluid_hbm,
+    velocity_hbm,
+    volume_hbm,
+    cells_hbm,
+    void_ref,
+    drag_ref,
     fluid_ref,
     velocity_ref,
     volume_ref,
     cells_ref,
-    void_ref,
-    drag_ref,
+    load_sem,
     spots,
     tile,
     wide,
@@ -68,17 +73,25 @@
             lax.rem(here_y + (dy + count_y), count_y),
         )
 
+    loads = [
+        pltpu.make_async_copy(source, target, load_sem.at[at])
+        for at, (source, target) in enumerate(
+            (
+                (cells_hbm, cells_ref),
+                (volume_hbm, volume_ref),
+                (fluid_hbm, fluid_ref),
+                (velocity_hbm, velocity_ref),
+            )
+        )
+    ]
+    for load in loads:
+        load.start()
     barrier = pltpu.get_barrier_semaphore()
     for direction in DIRECTIONS:
         pl.semaphore_signal(barrier, inc=1, device_id=neighbour(direction), device_id_type=MESH)
 
-    for side, j in enumerate((0, cells_y - 1)):
-        for k in range(3):
-            for i in range(cells_x):
-                flow_out_y[side, k * cells_x + i : k * cells_x + i + 1] = fluid_ref[k, i, j : j + 1]
-            for side_x, i in enumerate((0, cells_x - 1)):
-                flow_out_c[side_x * 2 + side, k : k + 1] = fluid_ref[k, i, j : j + 1]
-
+    loads[0].wait()
+    loads[1].wait()
     alive_below = jnp.broadcast_to(live_ref[...], (1, lanes))
     half = rows // 2
     width = pair * lanes
@@ -125,15 +138,28 @@
             weights = jnp.where(
                 both_ids == narrow_rows(cells // (2 * depth), 2 * half), split, zero
             )
-            totals[s % 2] = totals[s % 2] + lax.dot_general(
-                weights, spot, (((1,), (1,)), ((), ())), preferred_element_type=jnp.float32
-            )
+            for p in range(2):
+                totals[p] = totals[p] + lax.dot_general(
+                    weights,
+                    spot[p * depth : (p + 1) * depth],
+                    (((1,), (1,)), ((), ())),
+                    preferred_element_type=jnp.float32,
+                )
         return totals
 
-    totals = [jnp.zeros((2 * half, 2 * depth), jnp.float32)] * 2
+    totals = [jnp.zeros((2 * half, depth), jnp.float32)] * 2
     first = turns // 2
     for turn in range(first):
         totals = deposit(turn, totals)
+
+    loads[2].wait()
+    loads[3].wait()
+    for side, j in enumerate((0, cells_y - 1)):
+        for k in range(3):
+            for i in range(cells_x):
+                flow_out_y[side, k * cells_x + i : k * cells_x + i + 1] = fluid_ref[k, i, j : j + 1]
+            for side_x, i in enumerate((0, cells_x - 1)):
+                flow_out_c[side_x * 2 + side, k : k + 1] = fluid_ref[k, i, j : j + 1]
 
     pl.semaphore_wait(barrier, len(DIRECTIONS))
 
@@ -180,11 +206,9 @@
 
     for turn in range(first, turns):
         totals = deposit(turn, totals)
-    total = totals[0] + totals[1]
-    total = total[:half] + total[half:]
     evens, odds = pl.ds(0, half, stride=2), pl.ds(1, half, stride=2)
-    tile[evens] = total[:, :depth]
-    tile[odds] = total[:, depth:]
+    tile[evens] = totals[0][:half] + totals[0][half:]
+    tile[odds] = totals[1][:half] + totals[1][half:]
 
     band = 2 * wide_y
     top = (wide_x - 2) * wide_y
@@ -249,8 +273,8 @@
         [part[g * 8 : (g + 1) * 8] for g in range(half // 8) for part in parts], axis=0
     )
     high, low = halves(mixed)
-    fields[:, : 2 * depth] = high
-    fields[:, 2 * depth :] = low
+    fields[: 4 * half] = high
+    fields[4 * half :] = low
     for i in range(cells_x):
         start = (i + 1) * wide_y + 1
         void_ref[i] = tile[start : start + cells_y]
@@ -260,17 +284,14 @@
         sums = [jnp.zeros((8, width), jnp.float32) for _ in range(4)]
         for s in range(point_count):
             spot = spots[turn, s]
-            picked = jnp.dot(
-                fields[...],
-                jnp.concatenate([spot, spot], axis=0),
-                preferred_element_type=jnp.float32,
-            )
+            picked = jnp.dot(fields[...], spot, preferred_element_type=jnp.float32)
             row = jnp.broadcast_to(cell_rows(turn, s) // (2 * depth), (8, width))
             for g in range(half // 8):
                 hit = row == group_ids + 8 * g
                 for k in range(4):
                     at = (g * 4 + k) * 8
-                    sums[k] = sums[k] + jnp.where(hit, picked[at : at + 8], 0.0)
+                    value = picked[at : at + 8] + picked[4 * half + at : 4 * half + at + 8]
+                    sums[k] = sums[k] + jnp.where(hit, value, 0.0)
         share = shares(turn)
         weight_sum = jnp.sum(sums[3], axis=0, keepdims=True)
         for k in range(3):
@@ -304,13 +325,18 @@
             jax.ShapeDtypeStruct((cells_x, cells_y, depth), f32),
             jax.ShapeDtypeStruct((3, block_count, lanes), f32),
         ),
-        in_specs=[vmem] * 5,
+        in_specs=[vmem] + [pl.BlockSpec(memory_space=pltpu.HBM)] * 4,
         out_specs=(vmem, vmem),
         scratch_shapes=[
+            pltpu.VMEM(fluid_velocity.shape, f32),
+            pltpu.VMEM((3, block_count, lanes), f32),
+            pltpu.VMEM((block_count, lanes), f32),
+            pltpu.VMEM((point_count, block_count, lanes), jnp.int32),
+            pltpu.SemaphoreType.DMA((4,)),
             pltpu.VMEM((block_count // pair, point_count, 2 * depth, pair * lanes), jnp.bfloat16),
             pltpu.VMEM((rows, depth), f32),
             pltpu.VMEM((3, rows, depth), f32),
-            pltpu.VMEM((2 * rows, 4 * depth), jnp.bfloat16),
+            pltpu.VMEM((4 * rows, 2 * depth), jnp.bfloat16),
             pltpu.VMEM((2, band, depth), f32),
             pltpu.VMEM((2, sides, depth), f32),
             pltpu.VMEM((4, 8, depth), f32),
@@ -325,7 +351,9 @@
             pltpu.SemaphoreType.DMA((16,)),
             pltpu.SemaphoreType.DMA((16,)),
         ],
-        compiler_params=pltpu.CompilerParams(collective_id=0, has_side_effects=True),
+        compiler_params=pltpu.CompilerParams(
+            collective_id=0, has_side_effects=True, vmem_limit_bytes=16 * 1024 * 1024
+        ),
     )(
         live_blocks,
         fluid_velocity,

time: 23 us -> 19.8 us (0.86)
  Pallas kernels: 19.5 us -> 14.6 us
  local copies, waits for them, and re-layouts: 1.98 us -> 3.63 us
    pallas_call x1, Pallas kernels: 19.5 us -> 14.6 us  [body(): pl.pallas_call(functools.partial(kernel, sizes), out_shape=(jax.ShapeDtyp...]
    unnamed x4 -> x10, local copies, waits for them, and re-layouts: 1.98 us -> 3.63 us
where the time goes in v3:
time: 19.8 us; the launch traced here: 19.5 us
  Pallas kernels  14.6 us (74%)
  local copies, waits for them, and re-layouts  3.63 us (18%)
  between operations  1.31 us (7%)
    pallas_call x1, Pallas kernels, body(): pl.pallas_call(functools.partial(kernel, sizes), out_shape=(jax.ShapeDtyp...  14.6 us
    unnamed x10, local copies, waits for them, and re-layouts  3.63 us

profile of v3, /device:TPU:0, one launch (start us, length us, event | category | flops | bytes accessed | tf_op | source)
XLA Modules:
  0.0 19.5 jit_solution(18172871048920590719)
XLA Ops:
  0.6 0.0 copy-start.2
  1.3 0.0 copy-done.2
  1.3 0.0 copy-start
  1.3 0.9 %copy-done = f32[3,4,16,128]{3,2,1,0:T(8,128)S(1)} copy-done((f32[3,4,16,128]{3,2,1,0:T(8,128)S(1)}, f32[3,4,16,128]{3,2,1,0:T(8,128)}, u32[]{:S(2)}) %copy-start) | copy-done | bytes 98328
  2.2 0.0 copy-start.1
  2.2 0.8 %copy-done.1 = s32[1,1,4,29,128]{4,2,3,1,0:T(4,128)S(1)} copy-done((s32[1,1,4,29,128]{4,2,3,1,0:T(4,128)S(1)}, s32[1,1,4,29,128]{4,2,3,1,0:T(4,128)}, u32[]{:S(2)}) %copy-start.1) | copy-done | bytes 59416
  3.0 0.0 copy-start.3
  3.0 0.7 %copy-done.3 = f32[1,1,4,128]{3,2,1,0:T(4,128)S(1)} copy-done((f32[1,1,4,128]{3,2,1,0:T(4,128)S(1)}, f32[1,1,4,128]{3,2,1,0:T(4,128)}, u32[]{:S(2)}) %copy-start.3) | copy-done | bytes 2072
  3.7 14.6 %shard_map.68 = (f32[4,16,128]{2,1,0:T(8,128)S(1)}, f32[3,4,128]{2,1,0:T(4,128)S(1)}) custom-call(s32[1,1]{1,0:T(1,128)S(6)} %copy.9.live_ref, f32[3,4,16,128]{3,2,1,0:T(8,128)S(1)} %copy-done, f32[3,4,128]{2,1,0:T(4,128)S(1)} %bitcast.12, f32[4,128]{1,0:T(4,128)S(1)} %bitcast.13, s32[29,4,128]{2,1,0:T(4,128)S(1)} %bitcast.10), custom_call_target="tpu_custom_call" | custom-call | tf_op jit(solution)/shard_map/pallas_call | solution.py:322
  18.3 0.6 %copy.10 = f32[4,16,128]{2,1,0:T(8,128)} copy(f32[4,16,128]{2,1,0:T(8,128)S(1)} %get-tuple-element.8) | data formatting | bytes 65536
  18.9 0.6 %copy.11 = f32[1,1,4,3,128]{4,2,3,1,0:T(4,128)} copy(f32[1,1,4,3,128]{4,2,3,1,0:T(4,128)S(1)} %bitcast.11) | data formatting | bytes 12288
Async XLA Ops:
  0.6 0.7 %copy-start.2 = (f32[1,1,4,3,128]{4,2,3,1,0:T(4,128)S(1)}, f32[1,1,4,3,128]{4,2,3,1,0:T(4,128)}, u32[]{:S(2)}) copy-start(f32[1,1,4,3,128]{4,2,3,1,0:T(4,128)} %param.6) | copy-start | bytes 18436
  1.3 0.9 %copy-start = (f32[3,4,16,128]{3,2,1,0:T(8,128)S(1)}, f32[3,4,16,128]{3,2,1,0:T(8,128)}, u32[]{:S(2)}) copy-start(f32[3,4,16,128]{3,2,1,0:T(8,128)} %fluid_hbm.1) | copy-start | bytes 294916
  2.2 0.8 %copy-start.1 = (s32[1,1,4,29,128]{4,2,3,1,0:T(4,128)S(1)}, s32[1,1,4,29,128]{4,2,3,1,0:T(4,128)}, u32[]{:S(2)}) copy-start(s32[1,1,4,29,128]{4,2,3,1,0:T(4,128)} %param.8) | copy-start | bytes 178180
  3.0 0.7 %copy-start.3 = (f32[1,1,4,128]{3,2,1,0:T(4,128)S(1)}, f32[1,1,4,128]{3,2,1,0:T(4,128)}, u32[]{:S(2)}) copy-start(f32[1,1,4,128]{3,2,1,0:T(4,128)} %param.7) | copy-start | bytes 6148

commit v4 on v3

--- a/solution.py
+++ b/solution.py
@@ -322,8 +322,8 @@
     void_fraction, drag = pl.pallas_call(
         functools.partial(kernel, sizes),
         out_shape=(
-            jax.ShapeDtypeStruct((cells_x, cells_y, depth), f32),
-            jax.ShapeDtypeStruct((3, block_count, lanes), f32),
+            pltpu.VMEM((cells_x, cells_y, depth), f32),
+            pltpu.VMEM((3, block_count, lanes), f32),
         ),
         in_specs=[vmem] + [pl.BlockSpec(memory_space=pltpu.HBM)] * 4,
         out_specs=(vmem, vmem),
@@ -352,7 +352,7 @@
             pltpu.SemaphoreType.DMA((16,)),
         ],
         compiler_params=pltpu.CompilerParams(
-            collective_id=0, has_side_effects=True, vmem_limit_bytes=16 * 1024 * 1024
+            collective_id=0, has_side_effects=True
         ),
     )(
         live_blocks,

time: 19.8 us -> 17.8 us (0.90)
  local copies, waits for them, and re-layouts: 3.63 us -> 1.21 us
  Pallas kernels: 14.6 us -> 15.2 us
    unnamed x10 -> x2, local copies, waits for them, and re-layouts: 3.63 us -> 1.21 us
    pallas_call x1, Pallas kernels: 14.6 us -> 15.2 us  [body(): pl.pallas_call(functools.partial(kernel, sizes), out_shape=(pltpu.VMEM((c...]
where the time goes in v4:
time: 17.8 us; the launch traced here: 17.7 us
  Pallas kernels  15.2 us (85%)
  between operations  1.29 us (7%)
  local copies, waits for them, and re-layouts  1.21 us (7%)
    pallas_call x1, Pallas kernels, body(): pl.pallas_call(functools.partial(kernel, sizes), out_shape=(pltpu.VMEM((c...  15.2 us
    unnamed x2, local copies, waits for them, and re-layouts  1.21 us

profile of v4, /device:TPU:0, one launch (start us, length us, event | category | flops | bytes accessed | tf_op | source)
XLA Modules:
  0.0 17.7 jit_solution(73784961966229755)
XLA Ops:
  1.3 15.2 %shard_map.68 = (f32[4,16,128]{2,1,0:T(8,128)S(1)}, f32[3,4,128]{2,1,0:T(4,128)S(1)}) custom-call(s32[1,1]{1,0:T(1,128)S(6)} %copy.11.live_ref, f32[3,4,16,128]{3,2,1,0:T(8,128)} %fluid_hbm.1, f32[3,4,128]{2,1,0:T(4,128)} %bitcast.12, f32[4,128]{1,0:T(4,128)} %bitcast.13, s32[29,4,128]{2,1,0:T(4,128)} %bitcast.11), custom_call_target="tpu_custom_call" | custom-call | tf_op jit(solution)/shard_map/pallas_call | solution.py:322
  16.4 0.6 %copy.9 = f32[4,16,128]{2,1,0:T(8,128)} copy(f32[4,16,128]{2,1,0:T(8,128)S(1)} %get-tuple-element.6) | data formatting | bytes 65536
  17.1 0.6 %copy.10 = f32[1,1,4,3,128]{4,2,3,1,0:T(4,128)} copy(f32[1,1,4,3,128]{4,2,3,1,0:T(4,128)S(1)} %bitcast.10) | data formatting | bytes 12288
